TPU v7x, 32 devices: a whole 2x2x4 slice. The times are simulated.
32 devices in a mesh: dp: 4 (over y, core), seq: 8 (over z, x).
Axes of the slice: x: 2, y: 2, z: 4, core: 2. Of those that a mesh axis runs over, the one named last changes fastest.
Arguments:
- head_inputs: bfloat16 [4, 3072, 1024], P('dp', 'seq'), may hold values from -6 to 6
- gate_inputs: bfloat16 [4, 3072, 1024], P('dp', 'seq'), may hold values from -6 to 6
- state_proj: bfloat16 [4, 3072, 256], P('dp', 'seq'), may hold values from -2 to 2
- time_steps: float32 [4, 3072, 16], P('dp', 'seq'), may hold values from -4.7 to 4.7
- token_ids: int32 [4, 3072], P('dp', 'seq'), may hold values from 0 to 50279, as said below
- token_counts: int32 [4], replicated, may hold values from 1536 to 3072
- teacher_out: bfloat16 [4, 3072, 1024], P('dp', 'seq'), may hold values from -6 to 6
- out_weight: float32 [1024, 1024], P(('dp', 'seq')), may hold values from -0.1875 to 0.1875
- decay_log: float32 [16], replicated, may hold values from -6.5 to 1
- step_bias: float32 [16], replicated, may hold values from -5 to -3
- skip_gain: float32 [16], replicated, may hold values from 0.5 to 1.5
- norm_gain: float32 [1024], replicated, may hold values from 0.5 to 1.5
Outputs:
- losses: float32 [2], replicated
- new_weight: float32 [1024, 1024], P(('dp', 'seq'))
- new_decay: float32 [16], replicated
- new_bias: float32 [16], replicated
- new_skip: float32 [16], replicated
- new_gain: float32 [1024], replicated
Inputs may be any that keep to these rules, and one draw needn't show every extreme that they name: `token_ids`: in each sequence exactly one position, never the first, holds id 0.
All inputs are finite; a program needn't handle non-finite values.
Results may differ from a plain program's by a relative error of at most 0.0003.
Values may be sent and summed in bfloat16 or wider, within the bound.
No kernel may reach another device: no remote copies, remote signals or barrier semaphores. Data moves between devices by JAX's collectives and lax.ppermute only.
A program may use at most 192 MiB of HBM per device.

v0:
```python
import jax
import jax.numpy as jnp
from jax import lax
from jax.sharding import PartitionSpec as P

STEPS = 2


norm_floor = 1.0
clip_limit = 1.0
learn_rate = 8.0
highest = lax.Precision.HIGHEST
masked_low = -10000.0


def prefix(part, axis, combine, identity):
    place = lax.axis_index(axis)
    gathered = jax.tree.map(lambda a: lax.all_gather(a, axis), part)
    state = jax.tree.map(lambda a, e: jnp.zeros_like(a) + jnp.asarray(e, a.dtype), part, identity)

    def one(turn, state):
        return combine(
            state, jax.tree.map(lambda a: lax.dynamic_index_in_dim(a, turn, 0, False), gathered)
        )

    return lax.fori_loop(0, place, one, state)


def prefix_2(array, axis, join, neutral):
    count = lax.axis_size(axis)
    place = lax.axis_index(axis)
    ahead = count - 1 - place
    gathered = jax.tree.map(
        lambda a, kind: lax.all_gather(a.astype(kind), axis),
        array,
        jax.tree.map(lambda a: jnp.bfloat16 if a.dtype == jnp.float32 else a.dtype, array),
    )
    state = jax.tree.map(lambda a, e: jnp.zeros_like(a) + jnp.asarray(e, a.dtype), array, neutral)

    def one(turn, state):
        source = count - 1 - turn
        return join(
            state,
            jax.tree.map(
                lambda a, own: lax.dynamic_index_in_dim(a, source, 0, False).astype(own.dtype),
                gathered,
                array,
            ),
        )

    return lax.fori_loop(0, ahead, one, state)


def joined(part, axis, combine):
    gathered = jax.tree.map(lambda a: lax.all_gather(a, axis), part)

    def take(source):
        return jax.tree.map(lambda a: lax.dynamic_index_in_dim(a, source, 0, False), gathered)

    return lax.fori_loop(
        1, lax.axis_size(axis), lambda source, state: combine(state, take(source)), take(0)
    )


def step_sizes(decay_log, step_bias, step_raw):
    step_width = jax.nn.softplus(step_raw + step_bias[None, :])
    decay_sum = jnp.cumsum(step_width * (-jnp.exp(decay_log))[None, :], axis=0)
    return (step_width, decay_sum)


def mix_block(
    decay_log,
    step_bias,
    skip_gain,
    norm_gain,
    state_in,
    head_inputs,
    gate_inputs,
    b_proj,
    c_proj,
    step_raw,
    segment,
):
    positions = head_inputs.shape[0]
    head_count = decay_log.shape[0]
    step_width, decay_sum = step_sizes(decay_log, step_bias, step_raw)
    inputs_f = head_inputs.astype(jnp.float32).reshape(positions, head_count, -1)
    scaled = inputs_f * step_width[:, :, None]
    scores = jnp.dot(c_proj, b_proj.T, preferred_element_type=jnp.float32)
    position = jnp.arange(positions)
    allowed = (segment[:, None] == segment[None, :]) & (position[:, None] >= position[None, :])

    def one_head(head_data):
        head_sum, head_scaled = head_data
        spread = head_sum[:, None] - head_sum[None, :]
        decay_grid = jnp.exp(jnp.where(allowed, spread, masked_low))
        return jnp.dot(decay_grid * scores, head_scaled, precision=highest)

    intra_sum = jnp.transpose(
        lax.map(one_head, (decay_sum.T, jnp.transpose(scaled, (1, 0, 2)))), (1, 0, 2)
    )
    entry_decay = jnp.exp(decay_sum) * (segment == 0)[:, None]
    carried = (
        jnp.einsum("in,hpn->ihp", c_proj.astype(jnp.float32), state_in, precision=highest)
        * entry_decay[:, :, None]
    )
    mixed_out = intra_sum + carried + skip_gain[None, :, None] * inputs_f
    gated = mixed_out.reshape(positions, -1) * jax.nn.silu(gate_inputs.astype(jnp.float32))
    mean_square = jnp.mean(gated * gated, axis=1, keepdims=True)
    return gated * norm_gain[None, :] * lax.rsqrt(mean_square + norm_floor)


def state_block(decay_log, step_bias, head_inputs, b_proj, step_raw, segment):
    positions = head_inputs.shape[0]
    head_count = decay_log.shape[0]
    step_width, decay_sum = step_sizes(decay_log, step_bias, step_raw)
    final_sum = decay_sum[-1]
    same_doc = (segment == segment[-1])[:, None]
    tail_decay = jnp.exp(jnp.where(same_doc, final_sum[None, :] - decay_sum, masked_low))
    inputs_f = head_inputs.astype(jnp.float32).reshape(positions, head_count, -1)
    weighted = inputs_f * (step_width * tail_decay)[:, :, None]
    state_out = jnp.einsum("jhp,jn->hpn", weighted, b_proj.astype(jnp.float32), precision=highest)
    carry_out = jnp.exp(final_sum) * (segment[-1] == 0)
    return (carry_out, state_out)


def combine_states(earlier, later):
    return (earlier[0] * later[0], later[0][:, None, None] * earlier[1] + later[1])


def combine_sums(first_part, second_part):
    summed_up = first_part[5] + second_part[5]
    back_part = summed_up - first_part[5]
    lost_part = first_part[5] - (summed_up - back_part) + (second_part[5] - back_part)
    grads_part = tuple(
        (left_item + right_item for left_item, right_item in zip(first_part[:5], second_part[:5]))
    )
    return grads_part + (summed_up, first_part[6] + second_part[6] + lost_part)


def per_device(
    head_inputs,
    gate_inputs,
    state_proj,
    time_steps,
    token_ids,
    token_counts,
    teacher_out,
    out_weight,
    decay_log,
    step_bias,
    skip_gain,
    norm_gain,
):
    tok_rows = head_inputs.shape[1]
    inner_width = head_inputs.shape[2]
    state_size = state_proj.shape[2] // 2
    model_width = teacher_out.shape[2]
    head_count = decay_log.shape[0]
    head_size = inner_width // head_count
    inputs_local = head_inputs[0]
    gates_local = gate_inputs[0]
    b_proj = state_proj[0, :, :state_size]
    c_proj = state_proj[0, :, state_size:]
    raw_local = time_steps[0]
    segment = jnp.cumsum((token_ids[0] == 0).astype(jnp.int32))
    position = lax.axis_index("seq") * tok_rows + jnp.arange(tok_rows, dtype=jnp.int32)
    own_count = lax.dynamic_index_in_dim(token_counts, lax.axis_index("dp"), keepdims=False)
    scored = (position < own_count).astype(jnp.float32)
    total_count = jnp.sum(token_counts).astype(jnp.float32)
    target_f = teacher_out[0].astype(jnp.float32)
    identity = (
        jnp.ones((head_count,), jnp.float32),
        jnp.zeros((head_count, head_size, state_size), jnp.float32),
    )
    losses = []
    for step_index in range(STEPS):
        weight_b = out_weight.astype(jnp.bfloat16)

        def state_part(decay_arg, bias_arg):
            return state_block(decay_arg, bias_arg, inputs_local, b_proj, raw_local, segment)

        (carry_out, state_out), state_pull = jax.vjp(state_part, decay_log, step_bias)
        state_in = prefix((carry_out, state_out), "seq", combine_states, identity)[1]

        def mix_part(decay_arg, bias_arg, skip_arg, gain_arg, entering):
            return mix_block(
                decay_arg,
                bias_arg,
                skip_arg,
                gain_arg,
                entering,
                inputs_local,
                gates_local,
                b_proj,
                c_proj,
                raw_local,
                segment,
            )

        normed, mix_pull = jax.vjp(mix_part, decay_log, step_bias, skip_gain, norm_gain, state_in)
        normed_b = normed.astype(jnp.bfloat16)
        output = jnp.dot(
            normed_b,
            lax.all_gather(weight_b, ("dp", "seq"), axis=0, tiled=True),
            preferred_element_type=jnp.float32,
        )
        residual = output - target_f
        token_loss = jnp.sum(residual * residual, axis=1) * scored / model_width
        loss_part = jnp.sum(token_loss)
        out_grad = (residual * (2.0 / (model_width * total_count)) * scored[:, None]).astype(
            jnp.bfloat16
        )
        weight_grad = jnp.dot(normed_b.T, out_grad, preferred_element_type=jnp.float32)
        normed_grad = jnp.dot(
            out_grad,
            lax.all_gather(weight_b, ("dp", "seq"), axis=0, tiled=True).T,
            preferred_element_type=jnp.float32,
        )
        decay_one, bias_one, skip_grad, gain_grad, state_grad = mix_pull(normed_grad)
        after_grad = prefix_2((carry_out, state_grad), "seq", combine_states, identity)[1]
        carry_grad = jnp.sum(after_grad * state_in, axis=(1, 2))
        decay_two, bias_two = state_pull((carry_grad, after_grad))
        decay_grad = decay_one + decay_two
        bias_grad = bias_one + bias_two
        grad_rows = lax.psum_scatter(weight_grad, ("dp", "seq"), scatter_dimension=0, tiled=True)
        merged = joined(
            (
                decay_grad,
                bias_grad,
                skip_grad,
                gain_grad,
                jnp.sum(grad_rows * grad_rows),
                loss_part,
                jnp.zeros((), jnp.float32),
            ),
            ("dp", "seq"),
            combine_sums,
        )
        decay_grad, bias_grad, skip_grad, gain_grad = (merged[0], merged[1], merged[2], merged[3])
        norm_square = (
            merged[4]
            + jnp.sum(decay_grad * decay_grad)
            + jnp.sum(bias_grad * bias_grad)
            + jnp.sum(skip_grad * skip_grad)
            + jnp.sum(gain_grad * gain_grad)
        )
        losses.append((merged[5] + merged[6]) / total_count)
        factor = clip_limit / jnp.maximum(jnp.sqrt(norm_square), clip_limit)
        out_weight = out_weight - learn_rate * factor * grad_rows
        decay_log = decay_log - learn_rate * factor * decay_grad
        step_bias = step_bias - learn_rate * factor * bias_grad
        skip_gain = skip_gain - learn_rate * factor * skip_grad
        norm_gain = norm_gain - learn_rate * factor * gain_grad
    return (jnp.stack(losses), out_weight, decay_log, step_bias, skip_gain, norm_gain)


def solution(mesh):
    in_specs = (
        P("dp", "seq", None),
        P("dp", "seq", None),
        P("dp", "seq", None),
        P("dp", "seq", None),
        P("dp", "seq"),
        P(),
        P("dp", "seq", None),
        P(("dp", "seq"), None),
        P(),
        P(),
        P(),
        P(),
    )
    out_specs = (P(), P(("dp", "seq"), None), P(), P(), P(), P())
    return jax.shard_map(
        per_device, mesh=mesh, in_specs=in_specs, out_specs=out_specs, check_vma=False
    )
```

profile of v0, /device:TPU:10, one launch (start us, length us, event | category | flops | bytes accessed | tf_op | source)
XLA Modules:
  0.0 1181.2 jit_solution(14342196870966235500)
XLA Ops:
  17.6 2.9 convert_multiply_fusion.1
  26.7 3.3 copy.164
  31.3 4.6 broadcast.372.clone
  36.0 4.6 broadcast.372.clone.1
  40.6 72.0 %while.178 = (s32[]{:T(128)}, f32[16,384,64]{1,2,0:T(8,128)}, f32[16,384,384]{2,1,0:T(8,128)}, f32[16,384,384]{2,1,0:T(8,128)}, f32[16,384]{1,0:T(8,128)}, /*ind...) while((s32[]{:T(128)}, f32[16,384,64]{1,2,0:T(8,128)}, ...), condition=%wide.region_7.9_spmd.clone, body=%wide.region_6.8_spmd.clone.sunk | while | flops 115015680 | bytes 2674797 | solution.py:100
  45.9 2.5 fusion.225
  50.4 2.5 fusion.225
  59.4 2.5 fusion.225
  72.9 2.5 fusion.225
  95.3 2.5 fusion.225
  99.8 2.5 fusion.225
  104.3 2.5 fusion.225
  108.8 2.5 fusion.225
  117.2 3.1 copy.172
  120.3 14.3 %all-gather.12 = f32[8,1,16]{2,1,0:T(1,128)} all-gather(f32[1,1,16]{2,1,0:T(1,128)S(1)} %bitcast.743), channel_id=1, replica_groups=mesh['dp'=4,'seq'=8] {'seq'}, dimensions={0}, use_global_device_ids=true | all-gather | bytes 576 | tf_op jit(solution)/shard_map/all_gather | solution.py:18
  135.9 6.1 while.172
  142.1 5.4 multiply_reduce_fusion.7
  147.5 3.1 copy.165
  150.6 5.1 all-gather.23.cloned.1.call-done
  155.7 4.2 multiply_reduce_fusion.4
  165.7 3.1 copy.173
  168.7 2.9 convolution_convert_fusion.1
  171.9 18.6 %all-gather.13 = bf16[8,1,16]{2,1,0:T(2,128)(2,1)S(1)} all-gather(bf16[1,1,16]{2,1,0:T(2,128)(2,1)S(1)} %bitcast.745), channel_id=1, replica_groups=mesh['dp'=4,'seq'=8] {'seq'}, dimensions={0}, use_global_device_ids=true | all-gather | bytes 288 | tf_op jit(solution)/shard_map/all_gather | solution.py:34
  192.2 3.1 copy.167
  195.2 5.5 fusion.167
  202.1 71.3 %while.179 = (s32[]{:T(128)}, f32[16,384]{1,0:T(8,128)S(1)}, f32[16,384,64]{1,2,0:T(8,128)}, f32[16,384,64]{1,2,0:T(8,128)}, f32[16,384,64]{2,1,0:T(8,128)}, /*i...) while((s32[]{:T(128)}, f32[16,384]{1,0:T(8,128)S(1)}, ...), condition=%wide.region_15.17_spmd.clone, body=%wide.region_12.16_spmd.clone.sunk | while | flops 227672064 | bytes 2282125 | solution.py:100
  273.4 69.8 %all-gather.5 = f32[32768]{0:T(1024)S(1)} all-gather(f32[1024]{0:T(1024)S(1)} %get-tuple-element.1776), channel_id=7, replica_groups=mesh['dp'=4,'seq'=8] {'dp','seq'}, dimensions={0}, use_global_device_ids=true | all-gather | bytes 135168 | tf_op jit(solution)/shard_map/all_gather | solution.py:55
  346.2 3.7 reduce-window.55
  356.3 4.7 while.173
  363.5 3.7 reduce-window.59
  371.5 44.6 %all-reduce.14 = (f32[512]{0:T(512)S(1)}, f32[512]{0:T(512)S(1)}, f32[512]{0:T(512)S(1)}, f32[32]{0:T(128)S(1)}, f32[32]{0:T(128)S(1)}, /*index=5*/f32[32]{0:T(128)S(1)}) all-reduce(f32[512]{0:T(512)S(1)} %multiply_dynamic-update-slice_fusion.1, f32[512]{0:T(512)S(1)} %add_dynamic-update-slice_fusion.1, ...), channel_id=4, replica_groups=mesh['dp'=4,'seq'=8] {'dp','seq'}, use_global_device_ids=true, to_apply=%add.2 | all-reduce | flops 1632 | bytes 13056
  416.4 161.9 %while.174 = (s32[]{:T(128)}, f32[16]{0:T(128)S(1)}, f32[16]{0:T(128)S(1)}, f32[16]{0:T(128)S(1)}, f32[1024]{0:T(1024)S(1)}, /*index=5*/f32[]{:T(128)}, f32[]{:T...) while((s32[]{:T(128)}, f32[16]{0:T(128)S(1)}, ...), condition=%wide.region_38.40_spmd, body=%wide.region_37.39_spmd.sunk | while | flops 1086 | bytes 21427 | solution.py:60
  586.8 3.1 copy.180
  590.0 2.9 convert_multiply_fusion
  592.8 3.1 copy.181
  595.9 3.0 fusion.108
  600.3 3.4 copy.182
  605.9 4.6 broadcast.372
  610.5 4.6 broadcast.372.clone.2
  615.2 60.6 %while.180 = (s32[]{:T(128)}, f32[16,384,64]{1,2,0:T(8,128)}, f32[16,384,384]{2,1,0:T(8,128)}, f32[16,384,384]{2,1,0:T(8,128)}, f32[16,384]{1,0:T(8,128)S(1)}, /...) while((s32[]{:T(128)}, f32[16,384,64]{1,2,0:T(8,128)}, ...), condition=%wide.region_48.50_spmd.clone, body=%wide.region_47.49_spmd.clone.sunk | while | flops 115015680 | bytes 2674797 | solution.py:100
  618.9 2.5 fusion.233
  630.3 2.5 fusion.233
  664.3 2.5 fusion.233
  671.9 2.5 fusion.233
  677.0 3.1 copy.189
  680.1 13.2 %all-gather.14 = f32[8,1,16]{2,1,0:T(1,128)} all-gather(f32[1,1,16]{2,1,0:T(1,128)S(1)} %bitcast.744), channel_id=1, replica_groups=mesh['dp'=4,'seq'=8] {'seq'}, dimensions={0}, use_global_device_ids=true | all-gather | bytes 576 | tf_op jit(solution)/shard_map/all_gather | solution.py:18
  694.4 5.7 while.175
  700.2 5.5 multiply_reduce_fusion.3
  705.6 3.1 copy.183
  709.9 17.9 %all-gather.25.cloned.1.call-done = bf16[1024,1024]{1,0:T(8,128)(2,1)} async-done(((bf16[32,1024]{1,0:T(8,128)(2,1)}), bf16[1024,1024]{1,0:T(8,128)(2,1)}) %all-gather.25.cloned.1.call-update) | async-done | bytes 2097168 | tf_op jit(solution)/shard_map/all_gather | solution.py:205
  727.8 4.5 multiply_reduce_fusion
  738.5 3.1 copy.190
  741.6 2.9 convolution_convert_fusion
  744.8 15.2 %all-gather.15 = bf16[8,1,16]{2,1,0:T(2,128)(2,1)S(1)} all-gather(bf16[1,1,16]{2,1,0:T(2,128)(2,1)S(1)} %bitcast.746), channel_id=1, replica_groups=mesh['dp'=4,'seq'=8] {'seq'}, dimensions={0}, use_global_device_ids=true | all-gather | bytes 288 | tf_op jit(solution)/shard_map/all_gather | solution.py:34
  760.0 3.1 copy.184
  763.1 68.0 %all-gather.11 = f32[32768]{0:T(1024)S(1)} all-gather(f32[1024]{0:T(1024)S(1)} %copy-done.62), channel_id=13, replica_groups=mesh['dp'=4,'seq'=8] {'dp','seq'}, dimensions={0}, use_global_device_ids=true | all-gather | bytes 135168 | tf_op jit(solution)/shard_map/all_gather | solution.py:55
  833.8 5.0 fusion.169
  840.2 71.2 %while.181 = (s32[]{:T(128)}, f32[16,384]{1,0:T(8,128)S(1)}, f32[16,384,64]{1,2,0:T(8,128)}, f32[16,384,64]{1,2,0:T(8,128)}, f32[16,384,64]{2,1,0:T(8,128)}, /*i...) while((s32[]{:T(128)}, f32[16,384]{1,0:T(8,128)S(1)}, ...), condition=%wide.region_55.57_spmd.clone, body=%wide.region_52.56_spmd.clone.sunk | while | flops 227672064 | bytes 2282125 | solution.py:100
  911.5 3.7 reduce-window.65
  919.7 4.6 while.176
  926.0 3.7 reduce-window.69
  930.4 48.0 %reduce-scatter.5.cloned.1.call-done = f32[32,1024]{1,0:T(8,128)} async-done(((f32[1024,1024]{1,0:T(8,128)}), f32[32,1024]{1,0:T(8,128)}) %reduce-scatter.5.cloned.1.call-update) | async-done | bytes 131088 | tf_op jit(solution)/shard_map/reduce_scatter | solution.py:226
  980.7 44.4 %all-reduce.13 = (f32[512]{0:T(512)S(1)}, f32[512]{0:T(512)S(1)}, f32[512]{0:T(512)S(1)}, f32[32]{0:T(128)S(1)}, f32[32]{0:T(128)S(1)}) all-reduce(f32[512]{0:T(512)S(1)} %multiply_dynamic-update-slice_fusion, f32[512]{0:T(512)S(1)} %add_dynamic-update-slice_fusion, ...), channel_id=10, replica_groups=mesh['dp'=4,'seq'=8] {'dp','seq'}, use_global_device_ids=true, to_apply=%add.8 | all-reduce | flops 1600 | bytes 12800
  1025.4 138.9 %while.177 = (s32[]{:T(128)}, f32[16]{0:T(128)S(1)}, f32[16]{0:T(128)S(1)}, f32[16]{0:T(128)S(1)}, f32[1024]{0:T(1024)S(1)}, /*index=5*/f32[]{:T(128)}, f32[]{:T...) while((s32[]{:T(128)}, f32[16]{0:T(128)S(1)}, ...), condition=%wide.region_78.80_spmd, body=%wide.region_77.79_spmd.sunk | while | flops 1086 | bytes 21427 | solution.py:60
  (1058 shorter events, 488.2 us)
Async XLA Ops:
  7.2 128.7 %all-gather.27.cloned.1.call-start = ((), (), s32[]{:S(2)}) async-start(), calls=%async_computation.6 | async-start | bytes 4718592 | tf_op jit(solution)/shard_map/all_gather | solution.py:18
  8.5 7.3 copy-start.32
  10.4 5.4 copy-start.37
  11.1 2.6 copy-start.63
  13.0 333.1 %copy-start.28 = (f32[16,4]{0,1:T(4,128)}, f32[16,4]{0,1:T(4,128)S(1)}, u32[]{:S(2)}) copy-start(f32[16,4]{0,1:T(4,128)S(1)} %reduce-window.50) | copy-start | bytes 772
  13.7 158.0 %copy-start.25 = (f32[384,16]{0,1:T(8,128)}, f32[384,16]{0,1:T(8,128)S(1)}, u32[]{:S(2)}) copy-start(f32[384,16]{0,1:T(8,128)S(1)} %get-tuple-element.2006) | copy-start | bytes 73732
  24.1 131.6 %all-gather.23.cloned.1.call-start = ((), (), s32[]{:S(2)}) async-start(), calls=%async_computation.2 | async-start | bytes 2162688 | tf_op jit(solution)/shard_map/all_gather | solution.py:205
  24.8 331.5 %all-gather.29.cloned.1.call-start = ((), (), s32[]{:S(2)}) async-start(), calls=%async_computation.7 | async-start | bytes 2359296 | tf_op jit(solution)/shard_map/all_gather | solution.py:34
  40.6 72.0 %copy-start.5 = (bf16[1,384,1024]{2,1,0:T(8,128)(2,1)S(1)}, bf16[1,384,1024]{2,1,0:T(8,128)(2,1)}, u32[]{:S(2)}) copy-start(bf16[1,384,1024]{2,1,0:T(8,128)(2,1)} %param.34) | copy-start | bytes 2359300
  112.6 3.3 copy-start.26
  117.2 3.1 copy-start.65
  147.5 3.1 copy-start.56
  147.5 8.2 copy-start.43
  150.6 9.3 copy-start.68
  155.7 4.2 copy-start.12
  155.7 4.2 copy-start.74
  161.6 2.7 copy-start.8
  171.6 197.5 %reduce-scatter.3.cloned.1.call-start = ((), (), s32[]{:S(2)}) async-start(), calls=%async_computation.3 | async-start | bytes 4325376 | tf_op jit(solution)/shard_map/reduce_scatter | solution.py:226
  192.2 3.1 copy-start.69
  200.7 493.6 %all-gather.31.cloned.1.call-start = ((), (), s32[]{:S(2)}) async-start(), calls=%async_computation.8 | async-start | bytes 4718592 | tf_op jit(solution)/shard_map/all_gather | solution.py:18
  343.2 2.9 copy-start.23
  343.9 6.7 copy-start.45
  343.9 6.9 copy-start.67
  356.3 4.7 copy-start.14
  361.1 55.4 %slice-start = ((f32[32768]{0:T(1024)}), f32[1024]{0:T(1024)S(1)}, s32[]{:S(2)}) async-start(f32[32768]{0:T(1024)} %copy-done.23), calls=%async_computation.10 | async-start | bytes 8192 | tf_op jit(solution)/shard_map/jit(dynamic_index_in_dim)/dynamic_slice | solution.py:58
  362.0 7.1 copy-start.64
  362.0 9.5 copy-start.58
  362.0 221.5 %copy-start.48 = (f32[16]{0:T(128)S(1)}, f32[16]{0:T(128)}, u32[]{:S(2)}) copy-start(f32[16]{0:T(128)} %param.42) | copy-start | bytes 196
  362.0 223.5 %copy-start.39 = (pred[384]{0:T(512)(128)(4,1)S(1)}, pred[384]{0:T(512)(128)(4,1)}, u32[]{:S(2)}) copy-start(pred[384]{0:T(512)(128)(4,1)} %copy-done.37) | copy-start | bytes 1156
  578.4 8.5 copy-start.77
  583.5 3.4 copy-start.41
  585.2 4.8 copy-start.30
  585.6 90.2 %copy-start.27 = (f32[384,16]{0,1:T(8,128)}, f32[384,16]{0,1:T(8,128)S(1)}, u32[]{:S(2)}) copy-start(f32[384,16]{0,1:T(8,128)S(1)} %get-tuple-element.2004) | copy-start | bytes 73732
  586.8 3.1 copy-start.2
  592.8 3.1 copy-start.15
  598.9 128.9 %all-gather.25.cloned.1.call-start = ((), (), s32[]{:S(2)}) async-start(), calls=%async_computation.4 | async-start | bytes 2162688 | tf_op jit(solution)/shard_map/all_gather | solution.py:205
  600.3 3.4 copy-start.19
  600.3 3.4 copy-start.21
  604.3 315.3 %all-gather.33.cloned.1.call-start = ((), (), s32[]{:S(2)}) async-start(), calls=%async_computation.9 | async-start | bytes 2359296 | tf_op jit(solution)/shard_map/all_gather | solution.py:34
  677.0 16.2 %copy-start.73 = (f32[16]{0:T(128)S(1)}, f32[16]{0:T(128)}, u32[]{:S(2)}) copy-start(f32[16]{0:T(128)} %param.43) | copy-start | bytes 196
  677.0 16.8 %copy-start.44 = (f32[1024]{0:T(1024)S(1)}, f32[1024]{0:T(1024)}, u32[]{:S(2)}) copy-start(f32[1024]{0:T(1024)} %param.44) | copy-start | bytes 12292
  705.6 22.1 %copy-start.35 = (f32[1024]{0:T(1024)S(1)}, f32[1024]{0:T(1024)}, u32[]{:S(2)}) copy-start(f32[1024]{0:T(1024)} %multiply_subtract_fusion.3) | copy-start | bytes 12292
  727.8 4.5 copy-start.6
  727.8 4.5 copy-start.10
  727.8 4.5 copy-start.53
  727.8 4.5 copy-start.70
  727.8 4.5 copy-start.75
  734.5 2.7 copy-start.9
  738.5 3.1 copy-start.16
  741.6 3.0 copy-start.78
  744.5 233.9 %reduce-scatter.5.cloned.1.call-start = ((), (), s32[]{:S(2)}) async-start(), calls=%async_computation.5 | async-start | bytes 4325376 | tf_op jit(solution)/shard_map/reduce_scatter | solution.py:226
  760.0 3.1 copy-start.62
  831.2 2.6 copy-start.11
  840.2 71.2 %copy-start.31 = (f32[16,4]{0,1:T(4,128)S(1)}, f32[16,4]{0,1:T(4,128)}, u32[]{:S(2)}) copy-start(f32[16,4]{0,1:T(4,128)} %copy-done.30) | copy-start | bytes 772
  840.2 71.2 %copy-start.34 = (f32[384]{0:T(512)S(1)}, f32[384]{0:T(512)}, u32[]{:S(2)}) copy-start(f32[384]{0:T(512)} %copy-done.32) | copy-start | bytes 4612
  840.2 75.2 %copy-start.46 = (f32[1024]{0:T(1024)S(1)}, f32[1024]{0:T(1024)}, u32[]{:S(2)}) copy-start(f32[1024]{0:T(1024)} %get-tuple-element.1973) | copy-start | bytes 12292
  840.2 75.6 %copy-start.66 = (f32[384]{0:T(512)S(1)}, f32[384]{0:T(512)}, u32[]{:S(2)}) copy-start(f32[384]{0:T(512)} %get-tuple-element.2015) | copy-start | bytes 4612
  924.4 5.6 copy-start.60
  924.4 5.9 copy-start.61
  924.4 101.0 %slice-start.1 = ((f32[32768]{0:T(1024)}), f32[1024]{0:T(1024)S(1)}, s32[]{:S(2)}) async-start(f32[32768]{0:T(1024)} %copy-done.24), calls=%async_computation.11 | async-start | bytes 8192 | tf_op jit(solution)/shard_map/jit(dynamic_index_in_dim)/dynamic_slice | solution.py:58
  925.2 245.3 %copy-start.72 = (f32[16]{0:T(128)S(1)}, f32[16]{0:T(128)}, u32[]{:S(2)}) copy-start(f32[16]{0:T(128)} %multiply_subtract_fusion.7) | copy-start | bytes 196
  925.3 245.8 %copy-start.36 = (f32[1024]{0:T(1024)S(1)}, f32[1024]{0:T(1024)}, u32[]{:S(2)}) copy-start(f32[1024]{0:T(1024)} %multiply_subtract_fusion.3) | copy-start | bytes 12292
  925.3 247.0 %copy-start.20 = (f32[32,1024]{1,0:T(8,128)S(1)}, f32[32,1024]{1,0:T(8,128)}, u32[]{:S(2)}) copy-start(f32[32,1024]{1,0:T(8,128)} %param.40) | copy-start | bytes 393220
  925.3 247.0 %copy-start.22 = (f32[32,1024]{1,0:T(8,128)S(1)}, f32[32,1024]{1,0:T(8,128)}, u32[]{:S(2)}) copy-start(f32[32,1024]{1,0:T(8,128)} %reduce-scatter.3.cloned.1.call-done) | copy-start | bytes 393220
  (27 other events, 41.8 us)
Sparse Core Ops, SparseCore 0:
  24.2 72.6 all-gather.26
  100.5 55.1 all-gather.22
  171.8 54.2 all-gather.28
  228.2 138.3 reduce-scatter.2
  599.0 70.1 all-gather.30
  672.6 55.1 all-gather.24
  744.6 48.9 all-gather.32
  839.0 139.3 reduce-scatter.4
where the time goes:
time: 1200 us; the launch traced here: 1180 us
  blocking collectives  288 us (24%)
  matrix products  265 us (22%)
  local copies, waits for them, and re-layouts  237 us (20%)
  loops' own time  166 us (14%)
  other arithmetic  131 us (11%)
  waiting for transfers between devices  71.1 us (6%)
  between operations  22.6 us (2%)
    dot_general x96, matrix products, one_head(): return jnp.dot(decay_grid * scores, head_scaled, precision=highest)  220 us
    another operation x2, loops' own time, joined(): lax.fori_loop(1, lax.axis_size(axis), lambda source, state: combine(state...  164 us
    all_gather x2, blocking collectives, joined(): gathered = jax.tree.map(lambda a: lax.all_gather(a, axis), part)  138 us
    dynamic_slice x258, local copies, waits for them, and re-layouts, take(): lax.dynamic_index_in_dim(a, source, 0, False)  134 us
    unnamed x2, blocking collectives  89 us
    reduce_scatter x2, waiting for transfers between devices, per_device(): lax.psum_scatter(weight_grad, ('dp', 'seq'), scatter_dimension=0, tiled=T...  48 us
    dynamic_update_slice x32, other arithmetic, mix_block(): lax.map(one_head, (decay_sum.T, jnp.transpose(scaled, (1, 0, 2))))  40.7 us
    all_gather x2, blocking collectives, prefix_2(): lax.all_gather(a.astype(kind), axis)  33.7 us
  transfers between devices with their start and end apart: 8, of which 3 were waited for; matrix products, arithmetic and copies ran while one was open for 35% of the time, Pallas kernels for 0%

commit v1 on v0

v1 whole, which is shorter than its diff:
```python
import jax
import jax.numpy as jnp
from jax import lax
from jax.experimental import pallas as pl
from jax.experimental.pallas import tpu as pltpu
from jax.sharding import PartitionSpec as P

STEPS = 2


norm_floor = 1.0
clip_limit = 1.0
learn_rate = 8.0
highest = lax.Precision.HIGHEST
masked_low = -10000.0
bf16 = jnp.bfloat16
f32 = jnp.float32


def decay_matmul(left, right, sum_cols, sum_rows, seg_col, seg_row, values, reverse):
    tokens, width = values.shape
    heads = sum_cols.shape[1]
    head_size = width // heads
    group = max(1, 128 // head_size)
    lanes = group * head_size

    def kernel(left_ref, right_ref, cols_ref, rows_ref, sc_ref, sr_ref, val_ref, out_ref):
        scores = lax.dot_general(
            left_ref[...], right_ref[...], (((1,), (1,)), ((), ())), preferred_element_type=f32
        )
        row = lax.broadcasted_iota(jnp.int32, (tokens, tokens), 0)
        col = lax.broadcasted_iota(jnp.int32, (tokens, tokens), 1)
        order = (col >= row) if reverse else (row >= col)
        allowed = order & (sc_ref[...] == sr_ref[...])
        scores = jnp.where(allowed, scores, 0.0)
        lane = lax.broadcasted_iota(jnp.int32, (tokens, lanes), 1)
        for base in range(0, heads, group):
            piece = val_ref[:, base * head_size : base * head_size + lanes]
            result = None
            for inner in range(group):
                head = base + inner
                spread = cols_ref[:, head : head + 1] - rows_ref[head : head + 1, :]
                if reverse:
                    spread = -spread
                grid = (jnp.exp(jnp.minimum(spread, 0.0)) * scores).astype(bf16)
                part = jnp.dot(grid, piece, preferred_element_type=f32)
                result = part if result is None else jnp.where(lane >= inner * head_size, part, result)
            out_ref[:, base * head_size : base * head_size + lanes] = result

    return pl.pallas_call(
        kernel,
        out_shape=jax.ShapeDtypeStruct((tokens, width), f32),
        name="decay_back" if reverse else "decay_ahead",
    )(left, right, sum_cols, sum_rows, seg_col, seg_row, values)


def per_device(
    head_inputs,
    gate_inputs,
    state_proj,
    time_steps,
    token_ids,
    token_counts,
    teacher_out,
    out_weight,
    decay_log,
    step_bias,
    skip_gain,
    norm_gain,
):
    tok_rows = head_inputs.shape[1]
    inner_width = head_inputs.shape[2]
    state_size = state_proj.shape[2] // 2
    model_width = teacher_out.shape[2]
    head_count = decay_log.shape[0]
    head_size = inner_width // head_count
    blocks = lax.axis_size("seq")
    place = lax.axis_index("seq")
    x_b = head_inputs[0]
    x_f = x_b.astype(f32)
    b_proj = state_proj[0, :, :state_size]
    c_proj = state_proj[0, :, state_size:]
    raw = time_steps[0]
    token = jnp.arange(tok_rows, dtype=jnp.int32)
    starts = (token_ids[0] == 0).astype(jnp.int32)
    later = token[:, None] >= token[None, :]
    seg_col = jnp.sum(jnp.where(later, starts[None, :], 0), axis=1)[:, None]
    seg_row = jnp.sum(jnp.where(later.T, starts[:, None], 0), axis=0)[None, :]
    resets = jnp.sum(starts)
    lower = later.astype(f32)
    before_reset = (seg_col == 0).astype(f32)
    last_doc = seg_col == resets
    position = place * tok_rows + token
    own_count = lax.dynamic_index_in_dim(token_counts, lax.axis_index("dp"), keepdims=False)
    scored = (position < own_count).astype(f32)
    total_count = jnp.sum(token_counts).astype(f32)
    target_f = teacher_out[0].astype(f32)
    gate_f = gate_inputs[0].astype(f32)
    silu_gate = gate_f * jax.nn.sigmoid(gate_f)
    spread_mat = (
        jnp.arange(inner_width)[None, :] // head_size == jnp.arange(head_count)[:, None]
    ).astype(f32)

    def widen(a):
        return jnp.dot(a, spread_mat, precision=highest)

    def by_head(a):
        return lax.dot_general(a, spread_mat, (((1,), (1,)), ((), ())), precision=highest)

    index = jnp.arange(blocks)
    ahead_mask = (index[None, :] > index[:, None]) & (index[None, :] < place)
    back_mask = (index[None, :] < index[:, None]) & (index[None, :] > place)

    def block_weights(mask, valid, sums, counts):
        log_w = jnp.sum(jnp.where(mask[:, :, None], sums[None], 0.0), axis=1)
        hits = jnp.sum(jnp.where(mask, counts[None, :], 0.0), axis=1)
        return jnp.exp(log_w) * (valid & (hits == 0.0))[:, None].astype(f32)

    losses = []
    for step_index in range(STEPS):
        weight_all = lax.all_gather(out_weight.astype(bf16), ("dp", "seq"), axis=0, tiled=True)
        shifted = raw + step_bias[None, :]
        width = jax.nn.softplus(shifted)
        rate = width * (-jnp.exp(decay_log))[None, :]
        decay_sum = jnp.dot(lower, rate, precision=highest)
        sum_rows = decay_sum.T
        final_sum = decay_sum[-1]
        tail = jnp.exp(jnp.where(last_doc, final_sum[None, :] - decay_sum, masked_low))
        entry = widen(jnp.exp(decay_sum) * before_reset)
        width_wide = widen(width)
        tail_wide = widen(tail)
        scaled_f = x_f * width_wide
        scaled = scaled_f.astype(bf16)
        weighted = (scaled_f * tail_wide).astype(bf16)
        state_out = lax.dot_general(
            weighted, b_proj, (((0,), (0,)), ((), ())), preferred_element_type=f32
        )
        high = final_sum.astype(bf16)
        rest = final_sum - high.astype(f32)
        mid = rest.astype(bf16)
        low = (rest - mid.astype(f32)).astype(bf16)
        count_b = jnp.full((head_count,), resets, f32).astype(bf16)
        meta = jnp.stack([high, mid, low, count_b], axis=1)
        meta = jnp.pad(meta, ((0, 0), (0, state_size - 4)))
        gathered = lax.all_gather(jnp.concatenate([state_out.astype(bf16), meta], axis=0), "seq")
        meta_all = gathered[:, inner_width:, :4].astype(f32)
        sums_all = meta_all[:, :, 0] + meta_all[:, :, 1] + meta_all[:, :, 2]
        counts_all = meta_all[:, 0, 3]
        intra = decay_matmul(
            c_proj, b_proj, decay_sum, sum_rows, seg_col, seg_row, scaled, False
        )
        ahead = block_weights(ahead_mask, index < place, sums_all, counts_all)
        states = gathered[:, :inner_width].reshape(blocks, head_count, head_size, state_size)
        state_in = jnp.sum(states.astype(f32) * ahead[:, :, None, None], axis=0)
        state_in_b = state_in.reshape(inner_width, state_size).astype(bf16)
        carried = entry * lax.dot_general(
            c_proj, state_in_b, (((1,), (1,)), ((), ())), preferred_element_type=f32
        )
        mixed = intra + carried
        gated = (mixed + widen(skip_gain[None, :]) * x_f) * silu_gate
        scale = lax.rsqrt(jnp.mean(gated * gated, axis=1, keepdims=True) + norm_floor)
        unit = gated * scale
        normed_b = (unit * norm_gain[None, :]).astype(bf16)
        output = jnp.dot(normed_b, weight_all, preferred_element_type=f32)
        residual = output - target_f
        loss_part = jnp.sum(jnp.sum(residual * residual, axis=1) * scored) / model_width
        out_grad = (residual * (2.0 / (model_width * total_count)) * scored[:, None]).astype(bf16)
        weight_grad = lax.dot_general(
            normed_b, out_grad, (((0,), (0,)), ((), ())), preferred_element_type=f32
        )
        grad_rows = lax.psum_scatter(weight_grad, ("dp", "seq"), scatter_dimension=0, tiled=True)
        normed_grad = lax.dot_general(
            out_grad, weight_all, (((1,), (1,)), ((), ())), preferred_element_type=f32
        )
        gain_grad = jnp.sum(normed_grad * unit, axis=0)
        unit_grad = normed_grad * norm_gain[None, :]
        gated_grad = scale * (
            unit_grad - unit * jnp.mean(unit_grad * unit, axis=1, keepdims=True)
        )
        mixed_grad_f = gated_grad * silu_gate
        mixed_grad = mixed_grad_f.astype(bf16)
        rounded = mixed_grad.astype(f32)
        state_grad = lax.dot_general(
            (mixed_grad_f * entry).astype(bf16),
            c_proj,
            (((0,), (0,)), ((), ())),
            preferred_element_type=f32,
        )
        grads_all = lax.all_gather(state_grad.astype(bf16), "seq")
        intra_back = decay_matmul(
            b_proj, c_proj, decay_sum, sum_rows, seg_col, seg_row, mixed_grad, True
        )
        skip_grad = jnp.sum(by_head(jnp.sum(mixed_grad_f * x_f, axis=0, keepdims=True)), axis=0)
        back = block_weights(back_mask, index > place, sums_all, counts_all)
        grads_all = grads_all.reshape(blocks, head_count, head_size, state_size)
        after = jnp.sum(grads_all.astype(f32) * back[:, :, None, None], axis=0)
        carry_out = jnp.exp(final_sum) * (resets == 0)
        carry_grad = jnp.sum(after * state_in, axis=(1, 2)) * carry_out
        from_after = tail_wide * lax.dot_general(
            b_proj,
            after.reshape(inner_width, state_size).astype(bf16),
            (((1,), (1,)), ((), ())),
            preferred_element_type=f32,
        )
        back_near = by_head(intra_back * scaled.astype(f32))
        back_far = by_head(from_after * scaled_f)
        width_grad = by_head((intra_back + from_after) * x_f)
        sum_grad = by_head(rounded * mixed) - back_near - back_far
        rate_grad = lax.dot_general(lower, sum_grad, (((0,), (0,)), ((), ())), precision=highest)
        rate_grad = rate_grad + (jnp.sum(back_far, axis=0) + carry_grad)[None, :]
        decay_grad = jnp.sum(rate_grad * rate, axis=0)
        width_grad = width_grad + rate_grad * (-jnp.exp(decay_log))[None, :]
        bias_grad = jnp.sum(width_grad * jax.nn.sigmoid(shifted), axis=0)
        packed = jnp.concatenate(
            [
                gain_grad,
                decay_grad,
                bias_grad,
                skip_grad,
                jnp.sum(grad_rows * grad_rows)[None],
                loss_part[None],
            ]
        )
        merged = lax.psum(packed, ("dp", "seq"))
        small = merged[: inner_width + 3 * head_count]
        norm_square = merged[inner_width + 3 * head_count] + jnp.sum(small * small)
        losses.append(merged[inner_width + 3 * head_count + 1] / total_count)
        factor = clip_limit / jnp.maximum(jnp.sqrt(norm_square), clip_limit)
        change = learn_rate * factor
        out_weight = out_weight - change * grad_rows
        small = change * small
        norm_gain = norm_gain - small[:inner_width]
        decay_log = decay_log - small[inner_width : inner_width + head_count]
        step_bias = step_bias - small[inner_width + head_count : inner_width + 2 * head_count]
        skip_gain = skip_gain - small[inner_width + 2 * head_count :]
    return (jnp.stack(losses), out_weight, decay_log, step_bias, skip_gain, norm_gain)

def solution(mesh):
    in_specs = (
        P("dp", "seq", None),
        P("dp", "seq", None),
        P("dp", "seq", None),
        P("dp", "seq", None),
        P("dp", "seq"),
        P(),
        P("dp", "seq", None),
        P(("dp", "seq"), None),
        P(),
        P(),
        P(),
        P(),
    )
    out_specs = (P(), P(("dp", "seq"), None), P(), P(), P(), P())
    return jax.shard_map(
        per_device, mesh=mesh, in_specs=in_specs, out_specs=out_specs, check_vma=False
    )
```

time: 1200 us -> 751 us (0.63)
  waiting for transfers between devices: 71.1 us -> 501 us
  local copies, waits for them, and re-layouts: 237 us -> 16.1 us
  matrix products: 265 us -> 53.4 us
  blocking collectives: 288 us -> 90.2 us
  loops' own time: 166 us -> 0 us
  other arithmetic: 131 us -> 36.7 us
  Pallas kernels: 0 us -> 20.6 us
    reduce_scatter x2, waiting for transfers between devices: 48 us -> 264 us  [per_device(): lax.psum_scatter(weight_grad, ('dp', 'seq'), scatter_dimension=0, tiled=T...]
    all_gather x6, waiting for transfers between devices: 23 us -> 237 us  [the longest x2 98.4 us: per_device(): lax.all_gather(out_weight.astype(bf16), ('dp', 'seq'), axis=0, tiled=True)]
    dot_general x111 -> x36, matrix products: 265 us -> 53.4 us  [the longest x8 11 us: widen(): return jnp.dot(a, spread_mat, precision=highest)]
    all_gather x6 -> x0, blocking collectives: 199 us -> none  [the longest x2 138 us: joined(): gathered = jax.tree.map(lambda a: lax.all_gather(a, axis), part)]
    another operation x10 -> x0, loops' own time: 166 us -> none  [the longest x2 164 us: joined(): lax.fori_loop(1, lax.axis_size(axis), lambda source, state: combine(state...]
    dynamic_slice x290 -> x0, local copies, waits for them, and re-layouts: 146 us -> none  [the longest x258 134 us: take(): lax.dynamic_index_in_dim(a, source, 0, False)]
    psum x0 -> x2, blocking collectives: none -> 90.2 us  [per_device(): merged = lax.psum(packed, ('dp', 'seq'))]
    unnamed x2 -> x0, blocking collectives: 89 us -> none
  transfers between devices with their start and end apart: 8 -> 8, of which waited for: 3 -> 8; matrix products, arithmetic and copies ran while one was open for 35% -> 8% of each run, Pallas kernels for 0% -> 3%
where the time goes in v1:
time: 751 us; the launch traced here: 742 us
  waiting for transfers between devices  501 us (67%)
  blocking collectives  90.2 us (12%)
  matrix products  53.4 us (7%)
  other arithmetic  36.7 us (5%)
  between operations  23.2 us (3%)
  Pallas kernels  20.6 us (3%)
  local copies, waits for them, and re-layouts  16.1 us (2%)
    reduce_scatter x2, waiting for transfers between devices, per_device(): lax.psum_scatter(weight_grad, ('dp', 'seq'), scatter_dimension=0, tiled=T...  264 us
    all_gather x2, waiting for transfers between devices, per_device(): lax.all_gather(out_weight.astype(bf16), ('dp', 'seq'), axis=0, tiled=True)  98.4 us
    psum x2, blocking collectives, per_device(): merged = lax.psum(packed, ('dp', 'seq'))  90.2 us
    all_gather x2, waiting for transfers between devices, per_device(): lax.all_gather(jnp.concatenate([state_out.astype(bf16), meta], axis=0), '...  76.2 us
    all_gather x2, waiting for transfers between devices, per_device(): grads_all = lax.all_gather(state_grad.astype(bf16), 'seq')  62 us
    pallas_call x4, Pallas kernels, decay_matmul(): pl.pallas_call(kernel, out_shape=jax.ShapeDtypeStruct((tokens, width), f3...  20.6 us
  transfers between devices with their start and end apart: 8, of which 8 were waited for; matrix products, arithmetic and copies ran while one was open for 8% of the time, Pallas kernels for 3%

profile of v1, /device:TPU:10, one launch (start us, length us, event | category | flops | bytes accessed | tf_op | source)
XLA Modules:
  0.0 742.0 jit_solution(17875685003288088764)
XLA Ops:
  7.9 1.2 fusion.54
  9.2 1.4 fusion.117
  12.9 3.0 fusion.138
  15.9 0.9 fusion.67
  18.1 0.7 fusion.57
  19.6 0.8 broadcast_in_dim.212.sc_ref
  23.6 5.0 decay_ahead.2
  29.5 2.0 fusion.68
  31.5 37.2 %all-gather.15.cloned.1.call-done = bf16[8320,128]{1,0:T(8,128)(2,1)} async-done(((bf16[1040,128]{1,0:T(8,128)(2,1)}), bf16[8320,128]{1,0:T(8,128)(2,1)}) %all-gather.15.cloned.1.call-update) | async-done | bytes 2129936 | tf_op jit(solution)/shard_map/all_gather | solution.py:145
  68.7 0.8 slice.122
  70.3 3.3 multiply_reduce_fusion.1
  73.6 3.6 multiply_reduce_fusion.9
  77.3 49.3 %all-gather.11.cloned.1.call-done = bf16[1024,1024]{1,0:T(8,128)(2,1)} async-done(((bf16[32,1024]{1,0:T(8,128)(2,1)}), bf16[1024,1024]{1,0:T(8,128)(2,1)}) %all-gather.11.cloned.1.call-update) | async-done | bytes 2097168 | tf_op jit(solution)/shard_map/all_gather | solution.py:121
  126.5 3.0 multiply_reduce_fusion.6
  129.6 1.3 multiply_reduce_fusion.7
  130.9 0.8 fusion.8
  131.8 1.2 copy-done.7
  132.9 1.2 convolution_convert_fusion.2
  134.3 4.7 fusion.130
  140.5 1.0 convert_element_type.365.val_ref
  141.5 5.4 decay_back.2
  146.9 1.2 select_reduce_fusion.11
  148.9 2.4 fusion.27
  151.3 31.0 %all-gather.17.cloned.1.call-done = bf16[8192,128]{1,0:T(8,128)(2,1)} async-done(((bf16[1024,128]{1,0:T(8,128)(2,1)}), bf16[8192,128]{1,0:T(8,128)(2,1)}) %all-gather.17.cloned.1.call-update) | async-done | bytes 2097168 | tf_op jit(solution)/shard_map/all_gather | solution.py:189
  182.3 2.6 fusion.1
  185.8 1.0 copy-done.12
  186.8 1.0 fusion.139
  187.8 0.8 fusion.122
  188.7 0.9 fusion.40
  190.0 1.0 fusion.49
  191.0 131.8 %reduce-scatter.3.cloned.1.call-done = f32[32,1024]{1,0:T(8,128)} async-done(((f32[1024,1024]{1,0:T(8,128)}), f32[32,1024]{1,0:T(8,128)}) %reduce-scatter.3.cloned.1.call-update) | async-done | bytes 131088 | tf_op jit(solution)/shard_map/reduce_scatter | solution.py:171
  322.8 1.5 multiply_reduce_fusion.13
  325.0 45.5 %psum.14 = f32[1074]{0:T(1024)S(1)} all-reduce(f32[1074]{0:T(1024)S(1)} %concatenate.13), channel_id=1, replica_groups=mesh['dp'=4,'seq'=8] {'dp','seq'}, use_global_device_ids=true, to_apply=%region_23.24 | all-reduce | flops 1074 | bytes 8592 | tf_op jit(solution)/shard_map/psum | solution.py:224
  373.2 1.8 fusion.140
  375.8 0.9 fusion.64
  379.5 4.9 decay_ahead.3
  384.7 2.0 fusion.65
  386.8 39.0 %all-gather.19.cloned.1.call-done = bf16[8320,128]{1,0:T(8,128)(2,1)} async-done(((bf16[1040,128]{1,0:T(8,128)(2,1)}), bf16[8320,128]{1,0:T(8,128)(2,1)}) %all-gather.19.cloned.1.call-update) | async-done | bytes 2129936 | tf_op jit(solution)/shard_map/all_gather | solution.py:145
  425.8 0.8 slice.134
  427.3 3.3 multiply_reduce_fusion
  430.6 3.6 multiply_reduce_fusion.5
  434.3 49.2 %all-gather.13.cloned.1.call-done = bf16[1024,1024]{1,0:T(8,128)(2,1)} async-done(((bf16[32,1024]{1,0:T(8,128)(2,1)}), bf16[1024,1024]{1,0:T(8,128)(2,1)}) %all-gather.13.cloned.1.call-update) | async-done | bytes 2097168 | tf_op jit(solution)/shard_map/all_gather | solution.py:121
  483.4 3.0 multiply_reduce_fusion.2
  486.5 1.3 multiply_reduce_fusion.3
  487.8 0.8 fusion.12
  488.6 1.2 copy-done.9
  489.8 1.2 convolution_convert_fusion
  491.3 4.8 fusion.132
  497.5 1.0 convert_element_type.389.val_ref
  498.5 5.3 decay_back.3
  503.9 1.2 select_reduce_fusion.10
  505.9 2.4 fusion.18
  508.2 31.0 %all-gather.21.cloned.1.call-done = bf16[8192,128]{1,0:T(8,128)(2,1)} async-done(((bf16[1024,128]{1,0:T(8,128)(2,1)}), bf16[8192,128]{1,0:T(8,128)(2,1)}) %all-gather.21.cloned.1.call-update) | async-done | bytes 2097168 | tf_op jit(solution)/shard_map/all_gather | solution.py:189
  539.2 2.6 fusion
  542.7 1.0 copy-done.14
  543.7 1.0 fusion.141
  544.7 0.8 fusion.120
  545.6 0.9 fusion.46
  546.9 1.0 fusion.50
  548.0 132.3 %reduce-scatter.5.cloned.1.call-done = f32[32,1024]{1,0:T(8,128)} async-done(((f32[1024,1024]{1,0:T(8,128)}), f32[32,1024]{1,0:T(8,128)}) %reduce-scatter.5.cloned.1.call-update) | async-done | bytes 131088 | tf_op jit(solution)/shard_map/reduce_scatter | solution.py:171
  680.3 1.5 multiply_reduce_fusion.12
  682.6 44.7 %psum.15 = f32[1074]{0:T(1024)S(1)} all-reduce(f32[1074]{0:T(1024)S(1)} %concatenate.15), channel_id=1, replica_groups=mesh['dp'=4,'seq'=8] {'dp','seq'}, use_global_device_ids=true, to_apply=%region_44.45 | all-reduce | flops 1074 | bytes 8592 | tf_op jit(solution)/shard_map/psum | solution.py:224
  729.9 1.3 slice_subtract_fusion.2
  733.1 1.6 multiply_subtract_fusion
  (251 shorter events, 22.6 us)
Async XLA Ops:
  7.2 61.6 %all-gather.15.cloned.1.call-start = ((), (), s32[]{:S(2)}) async-start(), calls=%async_computation.6 | async-start | bytes 2396160 | tf_op jit(solution)/shard_map/all_gather | solution.py:145
  9.0 6.9 copy-start.43
  9.2 6.7 copy-start.34
  12.1 3.8 copy-start.53
  17.0 1.9 copy-start.38
  17.0 4.0 copy-start.74
  18.8 107.7 %all-gather.11.cloned.1.call-start = ((), (), s32[]{:S(2)}) async-start(), calls=%async_computation.2 | async-start | bytes 2162688 | tf_op jit(solution)/shard_map/all_gather | solution.py:121
  19.6 162.7 %all-gather.17.cloned.1.call-start = ((), (), s32[]{:S(2)}) async-start(), calls=%async_computation.7 | async-start | bytes 2359296 | tf_op jit(solution)/shard_map/all_gather | solution.py:189
  23.6 5.7 copy-start.72
  23.6 5.9 copy-start.44
  28.6 41.3 %copy-start.62 = (pred[8]{0:T(512)(128)(4,1)}, pred[8]{0:T(512)(128)(4,1)S(1)}, u32[]{:S(2)}) copy-start(pred[8]{0:T(512)(128)(4,1)S(1)} %iota_compare_fusion.28) | copy-start | bytes 28
  28.6 45.0 %copy-start.64 = (pred[8]{0:T(512)(128)(4,1)}, pred[8]{0:T(512)(128)(4,1)S(1)}, u32[]{:S(2)}) copy-start(pred[8]{0:T(512)(128)(4,1)S(1)} %iota_compare_fusion.29) | copy-start | bytes 28
  29.3 44.3 %copy-start.56 = (pred[8,8]{1,0:T(8,128)(4,1)}, pred[8,8]{1,0:T(8,128)(4,1)S(1)}, u32[]{:S(2)}) copy-start(pred[8,8]{1,0:T(8,128)(4,1)S(1)} %fusion.115) | copy-start | bytes 196
  29.3 44.3 %copy-start.58 = (pred[8,8]{1,0:T(8,128)(4,1)}, pred[8,8]{1,0:T(8,128)(4,1)S(1)}, u32[]{:S(2)}) copy-start(pred[8,8]{1,0:T(8,128)(4,1)S(1)} %fusion.114) | copy-start | bytes 196
  29.5 44.1 %copy-start.26 = (bf16[1,384,1024]{2,1,0:T(8,128)(2,1)S(1)}, bf16[1,384,1024]{2,1,0:T(8,128)(2,1)}, u32[]{:S(2)}) copy-start(bf16[1,384,1024]{2,1,0:T(8,128)(2,1)} %param.13) | copy-start | bytes 2359300
  31.5 42.1 %copy-start = (bf16[1,384,1024]{2,1,0:T(8,128)(2,1)S(1)}, bf16[1,384,1024]{2,1,0:T(8,128)(2,1)}, u32[]{:S(2)}) copy-start(bf16[1,384,1024]{2,1,0:T(8,128)(2,1)} %param.12) | copy-start | bytes 2359300
  70.3 3.3 copy-start.21
  73.6 3.7 copy-start.32
  73.6 52.9 %copy-start.49 = (f32[1024]{0:T(1024)S(1)}, f32[1024]{0:T(1024)}, u32[]{:S(2)}) copy-start(f32[1024]{0:T(1024)} %param.23) | copy-start | bytes 12292
  126.5 3.1 copy-start.28
  130.9 2.0 copy-start.22
  134.1 188.7 %reduce-scatter.3.cloned.1.call-start = ((), (), s32[]{:S(2)}) async-start(), calls=%async_computation.3 | async-start | bytes 4325376 | tf_op jit(solution)/shard_map/reduce_scatter | solution.py:171
  139.1 286.7 %all-gather.19.cloned.1.call-start = ((), (), s32[]{:S(2)}) async-start(), calls=%async_computation.8 | async-start | bytes 2396160 | tf_op jit(solution)/shard_map/all_gather | solution.py:145
  141.5 7.4 copy-start.15
  182.3 2.6 copy-start.33
  182.3 3.1 copy-start.2
  186.8 1.9 copy-start.18
  186.8 1.9 copy-start.37
  187.8 1.8 copy-start.47
  187.8 1.8 copy-start.55
  187.8 2.1 copy-start.6
  190.0 183.1 %copy-start.68 = (f32[16]{0:T(128)S(1)}, f32[16]{0:T(128)}, u32[]{:S(2)}) copy-start(f32[16]{0:T(128)} %param.20) | copy-start | bytes 196
  373.1 11.4 %copy-start.50 = (f32[1072]{0:T(1024)}, f32[1072]{0:T(1024)S(1)}, u32[]{:S(2)}) copy-start(f32[1072]{0:T(1024)S(1)} %slice_multiply_fusion.1) | copy-start | bytes 12868
  373.2 1.9 copy-start.51
  373.2 1.9 copy-start.60
  373.2 2.5 copy-start.67
  373.2 2.6 copy-start.54
  375.0 2.2 copy-start.13
  376.7 2.0 copy-start.39
  376.8 2.0 copy-start.41
  378.7 104.7 %all-gather.13.cloned.1.call-start = ((), (), s32[]{:S(2)}) async-start(), calls=%async_computation.4 | async-start | bytes 2162688 | tf_op jit(solution)/shard_map/all_gather | solution.py:121
  379.5 5.1 copy-start.73
  379.5 5.3 copy-start.46
  379.5 159.7 %all-gather.21.cloned.1.call-start = ((), (), s32[]{:S(2)}) async-start(), calls=%async_computation.9 | async-start | bytes 2359296 | tf_op jit(solution)/shard_map/all_gather | solution.py:189
  384.5 42.3 %copy-start.63 = (pred[8]{0:T(512)(128)(4,1)S(1)}, pred[8]{0:T(512)(128)(4,1)}, u32[]{:S(2)}) copy-start(pred[8]{0:T(512)(128)(4,1)} %copy-done.62) | copy-start | bytes 28
  384.5 42.3 %copy-start.65 = (pred[8]{0:T(512)(128)(4,1)S(1)}, pred[8]{0:T(512)(128)(4,1)}, u32[]{:S(2)}) copy-start(pred[8]{0:T(512)(128)(4,1)} %copy-done.64) | copy-start | bytes 28
  384.5 42.5 %copy-start.57 = (pred[8,8]{1,0:T(8,128)(4,1)S(1)}, pred[8,8]{1,0:T(8,128)(4,1)}, u32[]{:S(2)}) copy-start(pred[8,8]{1,0:T(8,128)(4,1)} %copy-done.56) | copy-start | bytes 196
  384.5 42.5 %copy-start.59 = (pred[8,8]{1,0:T(8,128)(4,1)S(1)}, pred[8,8]{1,0:T(8,128)(4,1)}, u32[]{:S(2)}) copy-start(pred[8,8]{1,0:T(8,128)(4,1)} %copy-done.58) | copy-start | bytes 196
  386.8 43.8 %copy-start.27 = (bf16[1,384,1024]{2,1,0:T(8,128)(2,1)S(1)}, bf16[1,384,1024]{2,1,0:T(8,128)(2,1)}, u32[]{:S(2)}) copy-start(bf16[1,384,1024]{2,1,0:T(8,128)(2,1)} %param.13) | copy-start | bytes 2359300
  427.3 3.3 copy-start.19
  430.6 3.7 copy-start.30
  483.4 3.1 copy-start.29
  487.8 2.0 copy-start.20
  491.0 189.3 %reduce-scatter.5.cloned.1.call-start = ((), (), s32[]{:S(2)}) async-start(), calls=%async_computation.5 | async-start | bytes 4325376 | tf_op jit(solution)/shard_map/reduce_scatter | solution.py:171
  498.5 7.4 copy-start.16
  539.2 2.7 copy-start.31
  539.2 3.1 copy-start.4
  543.7 1.9 copy-start.17
  543.7 1.9 copy-start.36
  544.7 1.8 copy-start.48
  544.7 2.1 copy-start.5
  546.9 183.0 %copy-start.69 = (f32[16]{0:T(128)S(1)}, f32[16]{0:T(128)}, u32[]{:S(2)}) copy-start(f32[16]{0:T(128)} %param.20) | copy-start | bytes 196
  546.9 186.2 %copy-start.40 = (f32[32,1024]{1,0:T(8,128)S(1)}, f32[32,1024]{1,0:T(8,128)}, u32[]{:S(2)}) copy-start(f32[32,1024]{1,0:T(8,128)} %param.19) | copy-start | bytes 393220
  546.9 186.2 %copy-start.42 = (f32[32,1024]{1,0:T(8,128)S(1)}, f32[32,1024]{1,0:T(8,128)}, u32[]{:S(2)}) copy-start(f32[32,1024]{1,0:T(8,128)} %reduce-scatter.3.cloned.1.call-done) | copy-start | bytes 393220
  (19 other events, 26.4 us)
Sparse Core Ops, SparseCore 0:
  19.0 49.7 all-gather.14
  71.7 54.7 all-gather.10
  134.2 48.0 all-gather.16
  184.5 138.2 reduce-scatter.2
  378.8 46.8 all-gather.18
  428.6 54.7 all-gather.12
  491.1 48.0 all-gather.20
  541.5 138.7 reduce-scatter.4
